TPU v7x, 8 devices: a whole 2x2x1 slice. The times are simulated.
8 devices in a mesh: replica: 1 (over z), model: 8 (over y, x, core).
Axes of the slice: x: 2, y: 2, z: 1, core: 2. Of those that a mesh axis runs over, the one named last changes fastest.
Arguments:
- x: bfloat16 [512, 2048], P('replica')
- w_query: bfloat16 [2048, 2048], P(None, 'model')
- w_key: bfloat16 [2048, 256], replicated
- w_value: bfloat16 [2048, 256], replicated
- w_out: bfloat16 [2048, 2048], P('model')
- k_cache: bfloat16 [512, 1, 2048, 256], P('replica')
- v_cache: bfloat16 [512, 1, 2048, 256], P('replica')
- lengths: int32 [512], P('replica')
Outputs:
- output 1: bfloat16 [512, 2048], P('replica')
- output 2: bfloat16 [512, 1, 256], P('replica')
- output 3: bfloat16 [512, 1, 256], P('replica')
All inputs are finite; a program needn't handle non-finite values.
Results may differ from a plain program's by a relative error of at most 0.00406014.
Values are sent between devices in bfloat16 or wider.
A program may use at most 4.25 GiB of HBM per device.

v0:
```python
import jax
import jax.numpy as jnp
from jax import lax
from jax.sharding import PartitionSpec as P


def attend(queries, k_rows, v_rows, k_one, v_one, seq_lens):
    inv_sqrt = queries.shape[-1] ** -0.5
    scores = jnp.einsum("bgrd,bgtd->bgrt", queries, k_rows, preferred_element_type=jnp.float32) * inv_sqrt
    score_new = jnp.einsum("bgrd,bgd->bgr", queries, k_one, preferred_element_type=jnp.float32) * inv_sqrt
    positions = jnp.arange(k_rows.shape[2])
    in_range = positions[None, None, None, :] < seq_lens[:, None, None, None]
    scores = jnp.where(in_range, scores, -jnp.inf)
    row_max = jnp.maximum(jnp.max(scores, axis=-1), score_new)
    weights = jnp.exp(scores - row_max[..., None])
    weight_new = jnp.exp(score_new - row_max)
    norm_sum = jnp.sum(weights, axis=-1) + weight_new
    out_sum = jnp.einsum("bgrt,bgtd->bgrd", weights.astype(jnp.bfloat16), v_rows, preferred_element_type=jnp.float32)
    out_sum = out_sum + weight_new.astype(jnp.bfloat16).astype(jnp.float32)[..., None] * v_one.astype(jnp.float32)[:, :, None, :]
    return (out_sum / norm_sum[..., None]).astype(jnp.bfloat16)


def solution(mesh):
    model_size = mesh.shape["model"]

    def local_step(x, w_query, w_key, w_value, w_out, k_cache, v_cache, lengths):
        batch_rows = x.shape[0]
        kv_heads = k_cache.shape[1]
        head_dim = k_cache.shape[3]
        local_rows = batch_rows // model_size
        row_start = lax.axis_index("model") * local_rows
        q_local = jnp.dot(x, w_query, preferred_element_type=jnp.float32).astype(jnp.bfloat16)
        q_rows = lax.all_to_all(q_local, "model", 0, 1, tiled=True)
        k_new = jnp.dot(x, w_key, preferred_element_type=jnp.float32).astype(jnp.bfloat16).reshape(batch_rows, kv_heads, head_dim)
        v_new = jnp.dot(x, w_value, preferred_element_type=jnp.float32).astype(jnp.bfloat16).reshape(batch_rows, kv_heads, head_dim)
        queries = q_rows.reshape(local_rows, kv_heads, -1, head_dim)
        out_rows = attend(
            queries,
            lax.dynamic_slice_in_dim(k_cache, row_start, local_rows, axis=0),
            lax.dynamic_slice_in_dim(v_cache, row_start, local_rows, axis=0),
            lax.dynamic_slice_in_dim(k_new, row_start, local_rows, axis=0),
            lax.dynamic_slice_in_dim(v_new, row_start, local_rows, axis=0),
            lax.dynamic_slice_in_dim(lengths, row_start, local_rows, axis=0),
        )
        out_heads = lax.all_to_all(out_rows.reshape(local_rows, -1), "model", 1, 0, tiled=True)
        part_sum = jnp.dot(out_heads, w_out, preferred_element_type=jnp.float32)
        full_sum = lax.psum(part_sum, "model")
        y = (x.astype(jnp.float32) + full_sum).astype(jnp.bfloat16)
        return y, k_new, v_new

    rows_spec = P("replica")
    return jax.shard_map(
        local_step,
        mesh=mesh,
        in_specs=(P("replica", None), P(None, "model"), P(), P(), P("model", None), rows_spec, rows_spec, rows_spec),
        out_specs=(rows_spec, rows_spec, rows_spec),
        check_vma=False,
    )
```

profile of v0, /device:TPU:0, one launch (start us, length us, event | category | flops | bytes accessed | tf_op | source)
XLA Modules:
  0.0 172.5 jit_solution(8191115867307554201)
XLA Ops:
  7.2 0.0 copy-start
  7.2 0.0 copy-start.1
  7.2 3.4 %convolution_convert_fusion.2 = bf16[512,256]{1,0:T(8,128)(2,1)} fusion(bf16[512,2048]{1,0:T(8,128)(2,1)} %param.8, bf16[2048,256]{1,0:T(8,128)(2,1)} %param.9), kind=kOutput, calls=%fused_computation.19 | convolution fusion | flops 537001984 | bytes 3407872 | tf_op jit(solution)/shard_map/dot_general | solution.py:32
  10.6 4.3 %all-to-all-start = ((bf16[8,64,256]{2,1,0:T(8,128)(2,1)}), bf16[8,64,256]{2,1,0:T(8,128)(2,1)S(1)}, u32[]{:S(2)}, u32[]{:S(2)}) async-start(bf16[8,64,256]{2,1,0:T(8,128)(2,1)} %bitcast.40), calls=%async_computation | async-start | bytes 524288 | tf_op jit(solution)/shard_map/all_to_all | solution.py:33
  14.9 0.0 all-reduce.2.cloned.1.call-start
  15.0 0.8 dynamic_slice.11
  15.7 0.1 iota_compare_fusion
  15.9 0.0 copy-done.1
  15.9 1.9 %convolution_convert_fusion.1 = bf16[512,256]{1,0:T(8,128)(2,1)S(1)} fusion(bf16[512,2048]{1,0:T(8,128)(2,1)S(1)} %copy-done.1, bf16[2048,256]{1,0:T(8,128)(2,1)} %param.10), kind=kOutput, calls=%fused_computation.18 | convolution fusion | flops 537001984 | bytes 3407872 | tf_op jit(solution)/shard_map/dot_general | solution.py:34
  17.8 0.0 copy-start.6
  17.8 2.0 %convolution_convert_fusion = bf16[512,256]{1,0:T(8,128)(2,1)S(1)} fusion(bf16[512,2048]{1,0:T(8,128)(2,1)S(1)} %copy-done.1, bf16[2048,256]{1,0:T(8,128)(2,1)} %param.11), kind=kOutput, calls=%fused_computation.17 | convolution fusion | flops 537001984 | bytes 3407872 | tf_op jit(solution)/shard_map/dot_general | solution.py:35
  19.9 0.0 copy-start.5
  19.9 0.7 dynamic-slice_bitcast_fusion
  20.5 0.0 copy-done.6
  20.5 0.0 copy-done.5
  20.6 0.6 dynamic-slice_convert_fusion
  21.2 0.4 all-to-all-done
  21.6 1.6 fusion.29
  23.2 28.5 %fusion.6 = (f32[64,8]{1,0:T(8,128)}, f32[64,8,2048]{2,1,0:T(8,128)}) fusion(pred[64,2048]{1,0:T(8,128)(4,1)S(1)} %iota_compare_fusion, bf16[512,1,2048,256]{3,2,1,0:T(8,128)(2,1)} %param.13, s32[]{:T(128)S(6)} %select_n.12, bf16[8,64,256]{2,1,0:T(8,128)(2,1)S(1)} %all-to-all-done), kind=kOutput, calls=%fused_computation.9 | convolution fusion | flops 540016128 | bytes 71698432 | tf_op jit(solution)/shard_map/bgrd,bgtd->bgrt/dot_general | solution.py:9
  51.8 0.0 copy-start.3
  51.8 0.0 copy-start.4
  51.8 0.8 multiply_maximum_fusion
  52.6 0.0 copy-start.2
  52.6 3.5 %fusion.7 = f32[64,8]{1,0:T(8,128)S(1)} fusion(f32[64,8,2048]{2,1,0:T(8,128)} %get-tuple-element.6, f32[64,8]{1,0:T(8,128)S(1)} %multiply_maximum_fusion, pred[64,2048]{1,0:T(8,128)(4,1)S(1)} %iota_compare_fusion), kind=kLoop, calls=%fused_computation.10 | loop fusion | flops 4193792 | bytes 4329472 | tf_op jit(solution)/shard_map/reduce_sum | solution.py:17
  56.1 0.0 copy-done.3
  56.1 0.0 copy-done.4
  56.1 0.6 convert_convert_fusion
  56.7 0.0 copy-done.2
  56.7 24.2 %fusion.24 = bf16[64,8,256]{2,1,0:T(8,128)(2,1)S(1)} fusion(bf16[512,1,2048,256]{3,2,1,0:T(8,128)(2,1)} %param.14, s32[]{:T(128)S(6)} %select_n.12, f32[64,8,2048]{2,1,0:T(8,128)} %get-tuple-element.6, f32[64,8]{1,0:T(8,128)} %copy-done.2, pred[64,2048]{1,0:T(8,128)(4,1)S(1)} %iota_compare_fusion, f32[64,8]{1,0:T(8,128)} %get-tuple-element.4, ...), kind=kOutput, calls=%fused_computation.21 | convolution fusion | flops 541589504 | bytes 71860224 | tf_op jit(solution)/shard_map/bgrt,bgtd->bgrd/dot_general | solution.py:18
  80.9 9.2 %all_to_all.32 = bf16[64,8,256]{2,0,1:T(8,128)(2,1)S(1)} all-to-all(bf16[64,8,256]{2,0,1:T(8,128)(2,1)S(1)} %copy.15), channel_id=1, replica_groups=mesh['replica'=1,'model'=8] {'model'}, dimensions={1} | all-to-all | bytes 524288 | tf_op jit(solution)/shard_map/all_to_all | solution.py:45
  90.1 0.0 copy-done
  90.1 2.7 %fusion.40 = f32[512,2048]{1,0:T(8,128)} fusion(bf16[512,256]{1,0:T(8,128)(2,1)S(1)} %bitcast.39, bf16[256,2048]{1,0:T(8,128)(2,1)S(1)} %copy-done), kind=kOutput, calls=%fused_computation.39 | convolution fusion | flops 536870912 | bytes 5505024 | tf_op jit(solution)/shard_map/dot_general | solution.py:46
  92.8 0.0 all-reduce.2.cloned.1.call-update
  92.8 68.5 %all-reduce.2.cloned.1.call-done = f32[512,2048]{1,0:T(8,128)} async-done(((f32[512,2048]{1,0:T(8,128)}), f32[512,2048]{1,0:T(8,128)}) %all-reduce.2.cloned.1.call-update) | async-done | bytes 4194320 | tf_op jit(solution)/shard_map/psum | solution.py:47
  161.4 4.2 %add_convert_fusion = bf16[512,2048]{1,0:T(8,128)(2,1)} fusion(f32[512,2048]{1,0:T(8,128)} %all-reduce.2.cloned.1.call-done, bf16[512,2048]{1,0:T(8,128)(2,1)S(1)} %copy-done.1), kind=kLoop, calls=%fused_computation.6 | loop fusion | flops 3145728 | bytes 8388608 | tf_op jit(solution)/shard_map/convert_element_type | solution.py:48
  (1 shorter events, 0.0 us)
Async XLA Ops:
  7.2 83.0 %copy-start = (bf16[256,2048]{1,0:T(8,128)(2,1)S(1)}, bf16[256,2048]{1,0:T(8,128)(2,1)}, u32[]{:S(2)}) copy-start(bf16[256,2048]{1,0:T(8,128)(2,1)} %param.12) | copy-start | bytes 3145732
  7.2 8.7 %copy-start.1 = (bf16[512,2048]{1,0:T(8,128)(2,1)S(1)}, bf16[512,2048]{1,0:T(8,128)(2,1)}, u32[]{:S(2)}) copy-start(bf16[512,2048]{1,0:T(8,128)(2,1)} %param.8) | copy-start | bytes 6291460
  10.6 11.0 %all-to-all-start = ((bf16[8,64,256]{2,1,0:T(8,128)(2,1)}), bf16[8,64,256]{2,1,0:T(8,128)(2,1)S(1)}, u32[]{:S(2)}, u32[]{:S(2)}) async-start(bf16[8,64,256]{2,1,0:T(8,128)(2,1)} %bitcast.40), calls=%async_computation | async-start | bytes 524288 | tf_op jit(solution)/shard_map/all_to_all | solution.py:33
  14.9 146.5 %all-reduce.2.cloned.1.call-start = ((), (), s32[]{:S(2)}) async-start(), calls=%async_computation.2 | async-start | bytes 8388608 | tf_op jit(solution)/shard_map/psum | solution.py:47
  17.8 2.7 %copy-start.6 = (bf16[512,256]{1,0:T(8,128)(2,1)}, bf16[512,256]{1,0:T(8,128)(2,1)S(1)}, u32[]{:S(2)}) copy-start(bf16[512,256]{1,0:T(8,128)(2,1)S(1)} %convolution_convert_fusion.1) | copy-start | bytes 786436
  19.9 0.7 copy-start.5
  51.8 4.3 %copy-start.3 = (f32[64,8]{1,0:T(8,128)S(1)}, f32[64,8]{1,0:T(8,128)}, u32[]{:S(2)}) copy-start(f32[64,8]{1,0:T(8,128)} %get-tuple-element.5) | copy-start | bytes 6148
  51.8 4.3 %copy-start.4 = (f32[64,1,8]{2,1,0:T(1,128)S(1)}, f32[64,1,8]{2,1,0:T(1,128)}, u32[]{:S(2)}) copy-start(f32[64,1,8]{2,1,0:T(1,128)} %fusion.29) | copy-start | bytes 6148
  52.6 4.1 %copy-start.2 = (f32[64,8]{1,0:T(8,128)}, f32[64,8]{1,0:T(8,128)S(1)}, u32[]{:S(2)}) copy-start(f32[64,8]{1,0:T(8,128)S(1)} %multiply_maximum_fusion) | copy-start | bytes 6148
Sparse Core Ops, SparseCore 0:
  93.0 68.3 all-reduce.1
where the time goes:
time: 173 us; the launch traced here: 172 us
  waiting for transfers between devices  69 us (40%)
  matrix products  64.4 us (37%)
  between operations  14.1 us (8%)
  other arithmetic  9.91 us (6%)
  blocking collectives  9.19 us (5%)
  starting transfers between devices  4.34 us (3%)
    psum x1, waiting for transfers between devices, local_step(): full_sum = lax.psum(part_sum, 'model')  68.5 us
    dot_general x1, matrix products, attend(): jnp.einsum('bgrd,bgtd->bgrt', queries, k_rows, preferred_element_type=jnp...  28.5 us
    dot_general x1, matrix products, attend(): jnp.einsum('bgrt,bgtd->bgrd', weights.astype(jnp.bfloat16), v_rows, prefe...  24.2 us
    all_to_all x1, blocking collectives, local_step(): lax.all_to_all(out_rows.reshape(local_rows, -1), 'model', 1, 0, tiled=True)  9.19 us
    all_to_all x1, starting transfers between devices, local_step(): q_rows = lax.all_to_all(q_local, 'model', 0, 1, tiled=True)  4.3 us
    convert_element_type x1, other arithmetic, local_step(): y = (x.astype(jnp.float32) + full_sum).astype(jnp.bfloat16)  4.22 us
  transfers between devices with their start and end apart: 2, of which 2 were waited for; matrix products, arithmetic and copies ran while one was open for 4% of the time, Pallas kernels for 0%

commit v1 on v0

v1 whole, which is shorter than its diff:
```python
import functools

import jax
import jax.numpy as jnp
from jax import lax
from jax.experimental import pallas as pl
from jax.experimental.pallas import tpu as pltpu
from jax.sharding import PartitionSpec as P

BF = jnp.bfloat16
F32 = jnp.float32
HEADS = 8
HD = 256
LOCAL = 64
SHORT = 32
GROUP = 16
CHUNK = 256
MAXLEN = 2048
SLOTS = 12
SCALE = HD ** -0.5
DIMS_T = (((1,), (1,)), ((), ()))


def coords():
    me = lax.axis_index("model")
    return me, me // 4, (me // 2) % 2, me % 2


def peer(rel):
    _, y, x, k = coords()
    dy, dx, dk = rel // 4, (rel // 2) % 2, rel % 2
    return (((y + dy) % 2) * 2 + (x + dx) % 2) * 2 + (k + dk) % 2


def entry_barrier(rels):
    barrier = pltpu.get_barrier_semaphore()
    for rel in rels:
        pl.semaphore_signal(barrier, inc=1, device_id={"model": peer(rel)}, device_id_type=pl.DeviceIdType.MESH)
    pl.semaphore_wait(barrier, len(rels))


def remote(src, dst, send_sem, recv_sem, rel):
    return pltpu.make_async_remote_copy(
        src_ref=src, dst_ref=dst, send_sem=send_sem, recv_sem=recv_sem,
        device_id={"model": peer(rel)}, device_id_type=pl.DeviceIdType.MESH)


RELS = (6, 7, 2, 3, 4, 5, 1)


def project_kernel(x_hbm, wq_hbm, wk_hbm, wv_hbm, wo_hbm, q_out, kn_out, vn_out, wc_out,
                   x_v, wq_v, wk_v, wv_v, q_v, in_sem, own_sem, qs, qr, ws, wr):
    me, y, x, k = coords()
    loads = [pltpu.make_async_copy(src, dst, in_sem.at[i]) for i, (src, dst) in enumerate(
        ((wq_hbm, wq_v), (x_hbm, x_v), (wk_hbm, wk_v), (wv_hbm, wv_v)))]
    for load in loads:
        load.start()
    own_w = pltpu.make_async_copy(
        wo_hbm.at[:, pl.ds(pl.multiple_of(me * HD, HD), HD)], wc_out.at[pl.ds(pl.multiple_of(me * HD, HD), HD), :], own_sem)
    own_w.start()
    entry_barrier(RELS)
    loads[0].wait()
    loads[1].wait()
    copies = []
    for chip_rel in (6, 2, 4, 0):
        chip = peer(chip_rel) // 2
        rows = pl.ds(pl.multiple_of(chip * 2 * LOCAL, 2 * LOCAL), 2 * LOCAL)
        q_v[rows, :] = jnp.dot(x_v[rows, :], wq_v[...], preferred_element_type=F32).astype(BF)
        for rel in (chip_rel, chip_rel + 1):
            if rel == 0:
                continue
            there = peer(rel)
            copy = remote(q_v.at[pl.ds(pl.multiple_of(there * LOCAL, LOCAL), LOCAL), :], q_out.at[me],
                          qs.at[rel], qr.at[rel], rel)
            copy.start()
            copies.append(copy)
    mine = pl.ds(pl.multiple_of(me * LOCAL, LOCAL), LOCAL)
    q_out[me] = q_v[mine, :]
    for rel in RELS:
        there = peer(rel)
        copy = remote(wo_hbm.at[:, pl.ds(pl.multiple_of(there * HD, HD), HD)],
                      wc_out.at[pl.ds(pl.multiple_of(me * HD, HD), HD), :], ws.at[rel], wr.at[rel], rel)
        copy.start()
        copies.append(copy)
    loads[2].wait()
    loads[3].wait()
    for part in range(2):
        rows = pl.ds(part * 256, 256)
        kn_out[rows, :] = jnp.dot(x_v[rows, :], wk_v[...], preferred_element_type=F32).astype(BF)
        vn_out[rows, :] = jnp.dot(x_v[rows, :], wv_v[...], preferred_element_type=F32).astype(BF)
    own_w.wait()
    for copy in copies:
        copy.wait()


def project(x, wq, wk, wv, wo):
    rows, depth = x.shape
    hbm_spec = pl.BlockSpec(memory_space=pltpu.HBM)
    vmem_spec = pl.BlockSpec(memory_space=pltpu.VMEM)
    return pl.pallas_call(
        project_kernel,
        out_shape=(
            jax.ShapeDtypeStruct((HEADS, LOCAL, HD), BF),
            jax.ShapeDtypeStruct((rows, HD), BF),
            jax.ShapeDtypeStruct((rows, HD), BF),
            jax.ShapeDtypeStruct((HEADS * HD, HD), BF),
        ),
        in_specs=[hbm_spec] * 5,
        out_specs=(vmem_spec,) * 4,
        scratch_shapes=[
            pltpu.VMEM((rows, depth), BF),
            pltpu.VMEM((depth, HD), BF),
            pltpu.VMEM((depth, HD), BF),
            pltpu.VMEM((depth, HD), BF),
            pltpu.VMEM((rows, HD), BF),
            pltpu.SemaphoreType.DMA((4,)),
            pltpu.SemaphoreType.DMA,
            pltpu.SemaphoreType.DMA((8,)),
            pltpu.SemaphoreType.DMA((8,)),
            pltpu.SemaphoreType.DMA((8,)),
            pltpu.SemaphoreType.DMA((8,)),
        ],
        compiler_params=pltpu.CompilerParams(collective_id=0, has_side_effects=True, vmem_limit_bytes=40 * 2 ** 20),
        name="project",
    )(x, wq, wk, wv, wo)


def attend_kernel(len_ref, q_ref, kn_ref, vn_ref, k_hbm, v_hbm, o_ref, kn_out, vn_out,
                  ks, vs, kl, vl, qf, knf, vnf, acc, lens_v, lidx, short_sem, k_sem, v_sem, new_sem):
    me = lax.axis_index("model")
    base = me * LOCAL
    short_k = pltpu.make_async_copy(k_hbm.at[pl.ds(base, LOCAL), 0, pl.ds(0, SHORT), :], ks, short_sem.at[0])
    short_v = pltpu.make_async_copy(v_hbm.at[pl.ds(base, LOCAL), 0, pl.ds(0, SHORT), :], vs, short_sem.at[1])
    short_k.start()
    short_v.start()
    new_k = pltpu.make_async_copy(kn_ref, kn_out, new_sem.at[0])
    new_v = pltpu.make_async_copy(vn_ref, vn_out, new_sem.at[1])

    def chunk_copy(cache, dst, sem, seq, slot, c):
        rows = pl.ds(pl.multiple_of(c * CHUNK, CHUNK), CHUNK)
        return pltpu.make_async_copy(cache.at[base + seq, 0, rows, :], dst.at[slot, rows, :], sem.at[slot])

    k_copy = functools.partial(chunk_copy, k_hbm, kl, k_sem)
    v_copy = functools.partial(chunk_copy, v_hbm, vl, v_sem)

    def fetch(seq, slot):
        chunks = (len_ref[base + seq] + CHUNK - 1) // CHUNK

        @pl.loop(0, chunks)
        def _(c):
            k_copy(seq, slot, c).start()
            v_copy(seq, slot, c).start()

    def scan(i, count):
        length = len_ref[base + i]
        lens_v[pl.ds(i, 1), :] = jnp.full((1, 128), length, jnp.int32)
        is_long = length > SHORT

        @pl.when(is_long)
        def _():
            lidx[count] = i

            @pl.when(count < SLOTS)
            def _():
                fetch(i, count)

        return count + is_long.astype(jnp.int32)

    n_long = lax.fori_loop(0, LOCAL, scan, jnp.int32(0))
    new_k.start()
    new_v.start()

    own = pl.ds(pl.multiple_of(base, LOCAL), LOCAL)
    qf[...] = q_ref[...].astype(F32)
    knf[...] = kn_ref[own, :].astype(F32)
    vnf[...] = vn_ref[own, :].astype(F32)

    short_k.wait()
    short_v.wait()
    col = lax.broadcasted_iota(jnp.int32, (GROUP, GROUP * SHORT), 1)
    row = lax.broadcasted_iota(jnp.int32, (GROUP, GROUP * SHORT), 0)
    same = (col // SHORT) == row
    slot_pos = col % SHORT
    for g in range(LOCAL // GROUP):
        seqs = pl.ds(g * GROUP, GROUP)
        qb = q_ref[:, seqs, :].reshape(HEADS * GROUP, HD)
        kb = ks[seqs].reshape(GROUP * SHORT, HD)
        vb = vs[seqs].reshape(GROUP * SHORT, HD)
        s = lax.dot_general(qb, kb, DIMS_T, preferred_element_type=F32) * SCALE
        valid = same & (slot_pos < lens_v[seqs, 0:1])
        s = jnp.where(valid[None], s.reshape(HEADS, GROUP, GROUP * SHORT), -jnp.inf)
        s_new = jnp.sum(qf[:, seqs, :] * knf[seqs, :][None], axis=-1, keepdims=True) * SCALE
        m = jnp.maximum(jnp.max(s, axis=-1, keepdims=True), s_new)
        e = jnp.exp(s - m)
        e_new = jnp.exp(s_new - m)
        total = jnp.sum(e, axis=-1, keepdims=True) + e_new
        num = jnp.dot(e.astype(BF).reshape(HEADS * GROUP, GROUP * SHORT), vb, preferred_element_type=F32)
        num = num.reshape(HEADS, GROUP, HD) + e_new.astype(BF).astype(F32) * vnf[seqs, :][None]
        acc[:, seqs, :] = num / total

    @pl.loop(0, n_long)
    def _(i):
        seq = lidx[i]
        slot = i % SLOTS
        length = len_ref[base + seq]
        chunks = (length + CHUNK - 1) // CHUNK
        at = pl.ds(seq, 1)
        for n in range(1, MAXLEN // CHUNK + 1):
            @pl.when(chunks == n)
            def _():
                for c in range(n):
                    k_copy(seq, slot, c).wait()
                q8 = jnp.concatenate([qf[h, at, :] for h in range(HEADS)], axis=0)
                s = lax.dot_general(q8.astype(BF), kl[slot, pl.ds(0, n * CHUNK), :], DIMS_T, preferred_element_type=F32) * SCALE
                pos = lax.broadcasted_iota(jnp.int32, s.shape, 1)
                s = jnp.where(pos < length, s, -jnp.inf)
                s_new = jnp.sum(q8 * knf[at, :], axis=-1, keepdims=True) * SCALE
                m = jnp.maximum(jnp.max(s, axis=-1, keepdims=True), s_new)
                e = jnp.exp(s - m)
                e_new = jnp.exp(s_new - m)
                total = jnp.sum(e, axis=-1, keepdims=True) + e_new
                for c in range(n):
                    v_copy(seq, slot, c).wait()
                num = jnp.dot(e.astype(BF), vl[slot, pl.ds(0, n * CHUNK), :], preferred_element_type=F32)
                num = num + e_new.astype(BF).astype(F32) * vnf[at, :]
                out = num / total
                for h in range(HEADS):
                    acc[h, at, :] = out[h:h + 1, :]

        @pl.when(i + SLOTS < n_long)
        def _():
            fetch(lidx[i + SLOTS], slot)

    o_ref[...] = acc[...].astype(BF)
    new_k.wait()
    new_v.wait()


def attend(lengths, q, k_new, v_new, k_cache, v_cache):
    rows = k_new.shape[0]
    any_spec = pl.BlockSpec(memory_space=pl.ANY)
    vmem_spec = pl.BlockSpec(memory_space=pltpu.VMEM)
    return pl.pallas_call(
        attend_kernel,
        out_shape=(
            jax.ShapeDtypeStruct((HEADS, LOCAL, HD), BF),
            jax.ShapeDtypeStruct((rows, HD), BF),
            jax.ShapeDtypeStruct((rows, HD), BF),
        ),
        in_specs=[pl.BlockSpec(memory_space=pltpu.SMEM), vmem_spec, vmem_spec, vmem_spec, any_spec, any_spec],
        out_specs=(vmem_spec, any_spec, any_spec),
        scratch_shapes=[
            pltpu.VMEM((LOCAL, SHORT, HD), BF),
            pltpu.VMEM((LOCAL, SHORT, HD), BF),
            pltpu.VMEM((SLOTS, MAXLEN, HD), BF),
            pltpu.VMEM((SLOTS, MAXLEN, HD), BF),
            pltpu.VMEM((HEADS, LOCAL, HD), F32),
            pltpu.VMEM((LOCAL, HD), F32),
            pltpu.VMEM((LOCAL, HD), F32),
            pltpu.VMEM((HEADS, LOCAL, HD), F32),
            pltpu.VMEM((LOCAL, 128), jnp.int32),
            pltpu.SMEM((LOCAL,), jnp.int32),
            pltpu.SemaphoreType.DMA((2,)),
            pltpu.SemaphoreType.DMA((SLOTS,)),
            pltpu.SemaphoreType.DMA((SLOTS,)),
            pltpu.SemaphoreType.DMA((2,)),
        ],
        compiler_params=pltpu.CompilerParams(vmem_limit_bytes=48 * 2 ** 20),
        cost_estimate=pl.CostEstimate(flops=2 * 10 ** 9, bytes_accessed=10 ** 7, transcendentals=10 ** 6),
        name="attend",
    )(lengths, q, k_new, v_new, k_cache, v_cache)


HALF = HEADS // 2
X, Y, D, S = 2, 4, 6, 1


def output_kernel(o_ref, wc_ref, x_hbm, y_ref, og, xc, load_sem, os, orr, ys, yr):
    me, _, _, k = coords()
    cols = pl.ds(pl.multiple_of(me * HD, HD), HD)
    load_x = pltpu.make_async_copy(x_hbm.at[:, cols], xc, load_sem)
    load_x.start()
    entry_barrier((X, Y, S))
    started = []

    def o_copy(owner_rel, half, to, index):
        owner = peer(owner_rel)
        part = pl.ds(0, HEADS) if half is None else pl.ds(half * HALF, HALF)
        ref = og.at[owner, part]
        return remote(o_ref.at[part] if owner_rel == 0 else ref, ref, os.at[index], orr.at[index], to)

    def go(copy):
        copy.start()
        started.append(copy)

    def recv_o(owner_rel, half, to, index):
        o_copy(owner_rel, half, to, index).wait_recv()

    go(o_copy(0, 0, X, 0))
    go(o_copy(0, 1, Y, 1))
    go(o_copy(0, 1, X, 2))
    go(o_copy(0, 0, Y, 3))
    go(o_copy(0, None, S, 4))

    og[me] = o_ref[...]
    load_x.wait()

    def y_copy(col_rel, chip_rel, core, to, index):
        column = peer(col_rel)
        chip = peer(chip_rel) // 2
        first = chip * 2 + (0 if core is None else core)
        rows = pl.ds(pl.multiple_of(first * LOCAL, LOCAL), LOCAL if core is not None else 2 * LOCAL)
        ref = y_ref.at[rows, pl.ds(pl.multiple_of(column * HD, HD), HD)]
        return remote(ref, ref, ys.at[index], yr.at[index], to)

    def compute(step, chip_rel):
        chip = peer(chip_rel) // 2
        total = jnp.zeros((2 * LOCAL, HD), F32)
        for h in range(HEADS):
            lhs = og[pl.ds(chip * 2, 2), h].reshape(2 * LOCAL, HD)
            total = total + jnp.dot(lhs, wc_ref[pl.ds(h * HD, HD), :], preferred_element_type=F32)
        rows = pl.ds(pl.multiple_of(chip * 2 * LOCAL, 2 * LOCAL), 2 * LOCAL)
        y_ref[rows, cols] = (xc[rows, :].astype(F32) + total).astype(BF)
        b = step * 11
        go(y_copy(0, chip_rel, 0, X, b + 0))
        go(y_copy(0, chip_rel, 1, Y, b + 1))
        go(y_copy(0, chip_rel, 1, X, b + 2))
        go(y_copy(0, chip_rel, 0, Y, b + 3))
        go(y_copy(0, chip_rel, None, S, b + 4))

    recv_o(S, None, S, 4)
    compute(0, 0)
    recv_o(X, 0, X, 0)
    go(o_copy(X, 0, Y, 5))
    recv_o(Y, 1, Y, 1)
    go(o_copy(Y, 1, X, 6))
    recv_o(X, 1, X, 2)
    go(o_copy(X, None, S, 7))
    recv_o(Y, 0, Y, 3)
    go(o_copy(Y, None, S, 8))
    recv_o(X + S, None, S, 7)
    compute(1, X)
    recv_o(Y + S, None, S, 8)
    compute(2, Y)
    recv_o(D, 0, Y, 5)
    go(o_copy(D, 0, S, 9))
    recv_o(D, 1, X, 6)
    go(o_copy(D, 1, S, 10))
    recv_o(D + S, 0, S, 9)
    recv_o(D + S, 1, S, 10)
    compute(3, D)

    def xor(a, b):
        return ((a // 4 + b // 4) % 2) * 4 + ((a // 2 + b // 2) % 2) * 2 + (a + b) % 2

    order = (0, X, Y, D)
    for step, rel in enumerate(order):
        b = step * 11
        at_x, at_y, at_d = xor(rel, X), xor(rel, Y), xor(rel, D)
        y_copy(X, at_x, 0, X, b + 0).wait_recv()
        go(y_copy(X, at_x, 0, Y, b + 5))
        y_copy(Y, at_y, 1, Y, b + 1).wait_recv()
        go(y_copy(Y, at_y, 1, X, b + 6))
        y_copy(X, at_x, 1, X, b + 2).wait_recv()
        go(y_copy(X, at_x, None, S, b + 7))
        y_copy(Y, at_y, 0, Y, b + 3).wait_recv()
        go(y_copy(Y, at_y, None, S, b + 8))
    for step, rel in enumerate(order):
        b = step * 11
        at_d = xor(rel, D)
        y_copy(D, at_d, 0, Y, b + 5).wait_recv()
        go(y_copy(D, at_d, 0, S, b + 9))
        y_copy(D, at_d, 1, X, b + 6).wait_recv()
        go(y_copy(D, at_d, 1, S, b + 10))
    for step, rel in enumerate(order):
        b = step * 11
        at_x, at_y, at_d = xor(rel, X), xor(rel, Y), xor(rel, D)
        y_copy(S, rel, None, S, b + 4).wait_recv()
        y_copy(X + S, at_x, None, S, b + 7).wait_recv()
        y_copy(Y + S, at_y, None, S, b + 8).wait_recv()
        y_copy(D + S, at_d, 0, S, b + 9).wait_recv()
        y_copy(D + S, at_d, 1, S, b + 10).wait_recv()
    for copy in started:
        copy.wait_send()


def output(o, wc, x):
    rows, width = x.shape
    hbm_spec = pl.BlockSpec(memory_space=pltpu.HBM)
    vmem_spec = pl.BlockSpec(memory_space=pltpu.VMEM)
    return pl.pallas_call(
        output_kernel,
        out_shape=jax.ShapeDtypeStruct((rows, width), BF),
        in_specs=[vmem_spec, vmem_spec, hbm_spec],
        out_specs=vmem_spec,
        scratch_shapes=[
            pltpu.VMEM((8, HEADS, LOCAL, HD), BF),
            pltpu.VMEM((rows, HD), BF),
            pltpu.SemaphoreType.DMA,
            pltpu.SemaphoreType.DMA((11,)),
            pltpu.SemaphoreType.DMA((11,)),
            pltpu.SemaphoreType.DMA((44,)),
            pltpu.SemaphoreType.DMA((44,)),
        ],
        compiler_params=pltpu.CompilerParams(collective_id=1, has_side_effects=True, vmem_limit_bytes=40 * 2 ** 20),
        name="output",
    )(o, wc, x)


def solution(mesh):
    def local_step(x, w_query, w_key, w_value, w_out, k_cache, v_cache, lengths):
        q, k_new, v_new, w_cols = project(x, w_query, w_key, w_value, w_out)
        o, k_new, v_new = attend(lengths, q, k_new, v_new, k_cache, v_cache)
        y = output(o, w_cols, x)
        return y, k_new[:, None, :], v_new[:, None, :]

    rows_spec = P("replica")
    return jax.shard_map(
        local_step,
        mesh=mesh,
        in_specs=(P("replica", None), P(None, "model"), P(), P(), P("model", None), rows_spec, rows_spec, rows_spec),
        out_specs=(rows_spec, rows_spec, rows_spec),
        check_vma=False,
    )
```

time: 173 us -> 62.1 us (0.36)
  waiting for transfers between devices: 69 us -> 0 us
  matrix products: 64.4 us -> 0 us
  Pallas kernels: 0 us -> 53.7 us
  between operations: 14.1 us -> 0.69 us
  other arithmetic: 9.91 us -> 0 us
  blocking collectives: 9.19 us -> 0 us
  local copies, waits for them, and re-layouts: 1.54 us -> 7.81 us
  starting transfers between devices: 4.34 us -> 0 us
    psum x1 -> x0, waiting for transfers between devices: 68.5 us -> none  [local_step(): full_sum = lax.psum(part_sum, 'model')]
    dot_general x7 -> x0, matrix products: 64.4 us -> none  [the longest x1 28.5 us: attend(): jnp.einsum('bgrd,bgtd->bgrt', queries, k_rows, preferred_element_type=jnp...]
    pallas_call x0 -> x3, Pallas kernels: none -> 53.7 us  [the longest x1 24.9 us: output(): pl.pallas_call(output_kernel, out_shape=jax.ShapeDtypeStruct((rows, width...]
    all_to_all x1 -> x0, blocking collectives: 9.19 us -> none  [local_step(): lax.all_to_all(out_rows.reshape(local_rows, -1), 'model', 1, 0, tiled=True)]
    unnamed x14 -> x15, local copies, waits for them, and re-layouts: 0.08 us -> 7.81 us
    convert_element_type x3 -> x0, other arithmetic: 5.47 us -> none  [the longest x1 4.22 us: local_step(): y = (x.astype(jnp.float32) + full_sum).astype(jnp.bfloat16)]
    all_to_all x1 -> x0, starting transfers between devices: 4.3 us -> none  [local_step(): q_rows = lax.all_to_all(q_local, 'model', 0, 1, tiled=True)]
    reduce_sum x1 -> x0, other arithmetic: 3.45 us -> none  [attend(): norm_sum = jnp.sum(weights, axis=-1) + weight_new]
  transfers between devices with their start and end apart: 2 -> 0, of which waited for: 2 -> 0; matrix products, arithmetic and copies ran while one was open for 4% -> 0% of each run, Pallas kernels for 0% -> 0%
where the time goes in v1:
time: 62.1 us; the launch traced here: 62.2 us
  Pallas kernels  53.7 us (86%)
  local copies, waits for them, and re-layouts  7.81 us (13%)
  between operations  0.69 us (1%)
    pallas_call x1, Pallas kernels, output(): pl.pallas_call(output_kernel, out_shape=jax.ShapeDtypeStruct((rows, width...  24.9 us
    pallas_call x1, Pallas kernels, project(): pl.pallas_call(project_kernel, out_shape=(jax.ShapeDtypeStruct((HEADS, LO...  20.8 us
    pallas_call x1, Pallas kernels, attend(): pl.pallas_call(attend_kernel, out_shape=(jax.ShapeDtypeStruct((HEADS, LOC...  7.97 us
    unnamed x15, local copies, waits for them, and re-layouts  7.81 us

profile of v1, /device:TPU:0, one launch (start us, length us, event | category | flops | bytes accessed | tf_op | source)
XLA Modules:
  0.0 62.2 jit_solution(12996474395067772745)
XLA Ops:
  0.6 0.0 copy-start
  0.6 1.6 %copy-done = bf16[512,2048]{1,0:T(8,128)(2,1)S(1)} copy-done((bf16[512,2048]{1,0:T(8,128)(2,1)S(1)}, bf16[512,2048]{1,0:T(8,128)(2,1)}, u32[]{:S(2)}) %copy-start) | copy-done | bytes 2097176
  2.2 0.0 copy-start.2
  2.2 1.2 %copy-done.2 = bf16[2048,256]{1,0:T(8,128)(2,1)S(1)} copy-done((bf16[2048,256]{1,0:T(8,128)(2,1)S(1)}, bf16[2048,256]{1,0:T(8,128)(2,1)}, u32[]{:S(2)}) %copy-start.2) | copy-done | bytes 1048600
  3.5 0.0 copy-start.3
  3.5 1.2 %copy-done.3 = bf16[2048,256]{1,0:T(8,128)(2,1)S(1)} copy-done((bf16[2048,256]{1,0:T(8,128)(2,1)S(1)}, bf16[2048,256]{1,0:T(8,128)(2,1)}, u32[]{:S(2)}) %copy-start.3) | copy-done | bytes 1048600
  4.7 0.0 copy-start.4
  4.7 1.2 %copy-done.4 = bf16[2048,256]{1,0:T(8,128)(2,1)S(1)} copy-done((bf16[2048,256]{1,0:T(8,128)(2,1)S(1)}, bf16[2048,256]{1,0:T(8,128)(2,1)}, u32[]{:S(2)}) %copy-start.4) | copy-done | bytes 1048600
  5.9 0.0 copy-start.5
  5.9 1.2 %copy-done.5 = bf16[256,2048]{1,0:T(8,128)(2,1)S(1)} copy-done((bf16[256,2048]{1,0:T(8,128)(2,1)S(1)}, bf16[256,2048]{1,0:T(8,128)(2,1)}, u32[]{:S(2)}) %copy-start.5) | copy-done | bytes 1048600
  7.1 0.0 copy-start.6
  7.1 20.8 %project.1 = (bf16[8,64,256]{2,1,0:T(8,128)(2,1)S(1)}, bf16[512,256]{1,0:T(8,128)(2,1)S(1)}, bf16[512,256]{1,0:T(8,128)(2,1)S(1)}, bf16[2048,256]{1,0:T(8,128)(2,1)S(1)}) custom-call(bf16[512,2048]{1,0:T(8,128)(2,1)S(1)} %copy-done, bf16[2048,256]{1,0:T(8,128)(2,1)S(1)} %copy-done.2, bf16[2048,256]{1,0:T(8,128)(2,1)S(1)} %copy-done.3, ...), custom_call_target="tpu_custom_call" | custom-call | tf_op jit(solution)/shard_map/project/pallas_call | solution.py:100
  27.9 0.0 copy-done.6
  27.9 0.0 copy-start.1
  27.9 8.0 %attend.1 = (bf16[8,64,256]{2,1,0:T(8,128)(2,1)S(1)}, bf16[512,256]{1,0:T(8,128)(2,1)}, bf16[512,256]{1,0:T(8,128)(2,1)}) custom-call(s32[512]{0:T(512)S(1)} %copy-done.6, bf16[8,64,256]{2,1,0:T(8,128)(2,1)S(1)} %get-tuple-element.10.q_ref, bf16[512,256]{1,0:T(8,128)(2,1)S(1)} %get-tuple-element.11.kn_ref, bf16[512,256]{1,0:T(8,128)(2,1)S(1)} %get-tuple-element.12.vn_ref, ...), custom_call_target="tpu_custom_call" | custom-call | flops 2000000000 | bytes 10000000 | tf_op jit(solution)/shard_map/attend/pallas_call | solution.py:243
  35.9 0.0 copy-done.1
  35.9 24.9 %output.1 = bf16[512,2048]{1,0:T(8,128)(2,1)S(1)} custom-call(bf16[8,64,256]{2,1,0:T(8,128)(2,1)S(1)} %get-tuple-element.13.o_ref, bf16[2048,256]{1,0:T(8,128)(2,1)S(1)} %get-tuple-element.14.wc_ref, bf16[512,2048]{1,0:T(8,128)(2,1)S(1)} %copy-done.1), custom_call_target="tpu_custom_call" | custom-call | tf_op jit(solution)/shard_map/output/pallas_call | solution.py:391
  60.9 1.3 %copy.12 = bf16[512,2048]{1,0:T(8,128)(2,1)} copy(bf16[512,2048]{1,0:T(8,128)(2,1)S(1)} %output.1) | data formatting | bytes 4194304
Async XLA Ops:
  0.6 1.6 %copy-start = (bf16[512,2048]{1,0:T(8,128)(2,1)S(1)}, bf16[512,2048]{1,0:T(8,128)(2,1)}, u32[]{:S(2)}) copy-start(bf16[512,2048]{1,0:T(8,128)(2,1)} %x_hbm.3) | copy-start | bytes 6291460
  2.2 1.2 %copy-start.2 = (bf16[2048,256]{1,0:T(8,128)(2,1)S(1)}, bf16[2048,256]{1,0:T(8,128)(2,1)}, u32[]{:S(2)}) copy-start(bf16[2048,256]{1,0:T(8,128)(2,1)} %wq_hbm.1) | copy-start | bytes 3145732
  3.5 1.2 %copy-start.3 = (bf16[2048,256]{1,0:T(8,128)(2,1)S(1)}, bf16[2048,256]{1,0:T(8,128)(2,1)}, u32[]{:S(2)}) copy-start(bf16[2048,256]{1,0:T(8,128)(2,1)} %wk_hbm.1) | copy-start | bytes 3145732
  4.7 1.2 %copy-start.4 = (bf16[2048,256]{1,0:T(8,128)(2,1)S(1)}, bf16[2048,256]{1,0:T(8,128)(2,1)}, u32[]{:S(2)}) copy-start(bf16[2048,256]{1,0:T(8,128)(2,1)} %wv_hbm.1) | copy-start | bytes 3145732
  5.9 1.2 %copy-start.5 = (bf16[256,2048]{1,0:T(8,128)(2,1)S(1)}, bf16[256,2048]{1,0:T(8,128)(2,1)}, u32[]{:S(2)}) copy-start(bf16[256,2048]{1,0:T(8,128)(2,1)} %wo_hbm.1) | copy-start | bytes 3145732
  7.1 20.8 %copy-start.6 = (s32[512]{0:T(512)S(1)}, s32[512]{0:T(512)}, u32[]{:S(2)}) copy-start(s32[512]{0:T(512)} %len_ref.1) | copy-start | bytes 6148
  27.9 8.0 %copy-start.1 = (bf16[512,2048]{1,0:T(8,128)(2,1)S(1)}, bf16[512,2048]{1,0:T(8,128)(2,1)}, u32[]{:S(2)}) copy-start(bf16[512,2048]{1,0:T(8,128)(2,1)} %x_hbm.3) | copy-start | bytes 6291460

commit v2 on v1

v2 whole, which is shorter than its diff:
```python
import jax
import jax.numpy as jnp
from jax import lax
from jax.experimental import pallas as pl
from jax.experimental.pallas import tpu as pltpu
from jax.sharding import PartitionSpec as P

BF = jnp.bfloat16
F32 = jnp.float32
HEADS = 8
HD = 256
LOCAL = 64
SHORT = 32
GROUP = 16
CHUNK = 256
MAXLEN = 2048
SLOTS = 14
HALFW = 128
MIB = 2 ** 20
SCALE = HD ** -0.5
DIMS_T = (((1,), (1,)), ((), ()))


def coords():
    me = lax.axis_index("model")
    return me, me // 4, (me // 2) % 2, me % 2


def peer(rel):
    _, y, x, k = coords()
    dy, dx, dk = rel // 4, (rel // 2) % 2, rel % 2
    return (((y + dy) % 2) * 2 + (x + dx) % 2) * 2 + (k + dk) % 2


def span(index, size):
    return pl.ds(pl.multiple_of(index * size, size), size)


def entry_barrier(rels):
    barrier = pltpu.get_barrier_semaphore()
    for rel in rels:
        pl.semaphore_signal(barrier, inc=1, device_id={"model": peer(rel)}, device_id_type=pl.DeviceIdType.MESH)
    pl.semaphore_wait(barrier, len(rels))


def remote(src, dst, send_sem, recv_sem, rel):
    return pltpu.make_async_remote_copy(
        src_ref=src, dst_ref=dst, send_sem=send_sem, recv_sem=recv_sem,
        device_id={"model": peer(rel)}, device_id_type=pl.DeviceIdType.MESH)


RELS = (6, 7, 2, 3, 4, 5, 1)


def softmax_parts(s, s_new):
    m = jnp.maximum(jnp.max(s, axis=-1, keepdims=True), s_new)
    e = jnp.exp(s - m)
    e_new = jnp.exp(s_new - m)
    total = jnp.sum(e, axis=-1, keepdims=True) + e_new
    return e.astype(BF), e_new.astype(BF).astype(F32), total


def project_kernel(len_ref, x_hbm, wq_hbm, wk_hbm, wv_hbm, wo_hbm, k_hbm, v_hbm, q_out, kn_out, vn_out, wc_out, o_out,
                   x_v, wq_v, wk_v, wv_v, q_v, ks, vs, lens_v, in_sem, own_sem, qs, qr, ws, wr):
    me, y, x, k = coords()
    mine = span(me, LOCAL)
    loads = [pltpu.make_async_copy(src, dst, in_sem.at[i]) for i, (src, dst) in enumerate((
        (wq_hbm, wq_v),
        (x_hbm, x_v),
        (wk_hbm, wk_v),
        (wv_hbm, wv_v),
        (k_hbm.at[mine, 0, pl.ds(0, SHORT), :], ks),
        (v_hbm.at[mine, 0, pl.ds(0, SHORT), :], vs),
    ))]
    loads[0].start()
    loads[1].start()
    entry_barrier(RELS)
    loads[0].wait()
    loads[1].wait()
    q_copies, w_copies = [], []
    for chip_rel in (6, 2, 4, 0):
        rows = span(peer(chip_rel) // 2, 2 * LOCAL)
        q_v[rows, :] = jnp.dot(x_v[rows, :], wq_v[...], preferred_element_type=F32).astype(BF)
        for rel in (chip_rel, chip_rel + 1):
            if rel == 0:
                continue
            copy = remote(q_v.at[span(peer(rel), LOCAL), :], q_out.at[me], qs.at[rel], qr.at[rel], rel)
            copy.start()
            q_copies.append(copy)
    for rel in RELS:
        copy = remote(wo_hbm.at[:, span(peer(rel), HD)], wc_out.at[span(me, HD), :], ws.at[rel], wr.at[rel], rel)
        copy.start()
        w_copies.append(copy)
    own_w = pltpu.make_async_copy(wo_hbm.at[:, span(me, HD)], wc_out.at[span(me, HD), :], own_sem)
    own_w.start()
    for load in loads[2:]:
        load.start()
    q_out[me] = q_v[mine, :]

    def spread(i, carry):
        lens_v[pl.ds(i, 1), :] = jnp.full((1, 128), len_ref[me * LOCAL + i], jnp.int32)
        return carry

    lax.fori_loop(0, LOCAL, spread, 0)
    for load in loads[2:]:
        load.wait()
    for part in range(2):
        rows = pl.ds(part * 256, 256)
        kn_out[rows, :] = jnp.dot(x_v[rows, :], wk_v[...], preferred_element_type=F32).astype(BF)
        vn_out[rows, :] = jnp.dot(x_v[rows, :], wv_v[...], preferred_element_type=F32).astype(BF)
    for copy in q_copies:
        copy.wait()

    width = GROUP * SHORT
    col = lax.broadcasted_iota(jnp.int32, (GROUP, width), 1)
    same = (col // SHORT) == lax.broadcasted_iota(jnp.int32, (GROUP, width), 0)
    slot_pos = col % SHORT

    def group(g, carry):
        seqs = span(g, GROUP)
        new = pl.ds(pl.multiple_of(me * LOCAL + g * GROUP, GROUP), GROUP)
        qg = q_out[:, seqs, :]
        s = lax.dot_general(qg.reshape(HEADS * GROUP, HD), ks[seqs].reshape(width, HD), DIMS_T, preferred_element_type=F32) * SCALE
        valid = same & (slot_pos < lens_v[seqs, 0:1])
        s = jnp.where(valid[None], s.reshape(HEADS, GROUP, width), -jnp.inf)
        s_new = jnp.sum(qg.astype(F32) * kn_out[new, :].astype(F32)[None], axis=-1, keepdims=True) * SCALE
        e, e_new, total = softmax_parts(s, s_new)
        num = jnp.dot(e.reshape(HEADS * GROUP, width), vs[seqs].reshape(width, HD), preferred_element_type=F32)
        num = num.reshape(HEADS, GROUP, HD) + e_new * vn_out[new, :].astype(F32)[None]
        o_out[:, seqs, :] = (num / total).astype(BF)
        return carry

    lax.fori_loop(0, LOCAL // GROUP, group, 0)
    own_w.wait()
    for copy in w_copies:
        copy.wait()


def project(lengths, x, wq, wk, wv, wo, k_cache, v_cache):
    rows, depth = x.shape
    hbm_spec = pl.BlockSpec(memory_space=pltpu.HBM)
    vmem_spec = pl.BlockSpec(memory_space=pltpu.VMEM)
    return pl.pallas_call(
        project_kernel,
        out_shape=(
            jax.ShapeDtypeStruct((HEADS, LOCAL, HD), BF),
            jax.ShapeDtypeStruct((rows, HD), BF),
            jax.ShapeDtypeStruct((rows, HD), BF),
            jax.ShapeDtypeStruct((HEADS * HD, HD), BF),
            jax.ShapeDtypeStruct((HEADS, LOCAL, HD), BF),
        ),
        in_specs=[pl.BlockSpec(memory_space=pltpu.SMEM)] + [hbm_spec] * 7,
        out_specs=(vmem_spec,) * 5,
        scratch_shapes=[
            pltpu.VMEM((rows, depth), BF),
            pltpu.VMEM((depth, HD), BF),
            pltpu.VMEM((depth, HD), BF),
            pltpu.VMEM((depth, HD), BF),
            pltpu.VMEM((rows, HD), BF),
            pltpu.VMEM((LOCAL, SHORT, HD), BF),
            pltpu.VMEM((LOCAL, SHORT, HD), BF),
            pltpu.VMEM((LOCAL, 128), jnp.int32),
            pltpu.SemaphoreType.DMA((6,)),
            pltpu.SemaphoreType.DMA,
            pltpu.SemaphoreType.DMA((8,)),
            pltpu.SemaphoreType.DMA((8,)),
            pltpu.SemaphoreType.DMA((8,)),
            pltpu.SemaphoreType.DMA((8,)),
        ],
        compiler_params=pltpu.CompilerParams(collective_id=0, has_side_effects=True, vmem_limit_bytes=24 * MIB),
        name="project",
    )(lengths, x, wq, wk, wv, wo, k_cache, v_cache)


def attend_kernel(len_ref, q_ref, kn_ref, vn_ref, os_ref, k_hbm, v_hbm, o_ref, kn_out, vn_out,
                  kl, vl, qf, knf, vnf, acc, lidx, k_sem, v_sem, new_sem):
    me = lax.axis_index("model")
    base = me * LOCAL
    new_k = pltpu.make_async_copy(kn_ref, kn_out, new_sem.at[0])
    new_v = pltpu.make_async_copy(vn_ref, vn_out, new_sem.at[1])

    def chunks_of(i):
        return (len_ref[base + lidx[i]] + CHUNK - 1) // CHUNK

    def each_part(i, action):
        slot = i % SLOTS
        chunks = chunks_of(i)
        first = jnp.int32(0)
        for size in (8, 4, 2, 1):
            take = chunks - first >= size
            rows = pl.ds(pl.multiple_of(first * CHUNK, CHUNK), size * CHUNK)

            @pl.when(take)
            def _():
                for cache, dst, sem in ((k_hbm, kl, k_sem), (v_hbm, vl, v_sem)):
                    for half in range(2):
                        action(pltpu.make_async_copy(
                            cache.at[base + lidx[i], 0, rows, pl.ds(half * HALFW, HALFW)],
                            dst.at[slot, half, rows, :], sem.at[slot]))

            first = first + jnp.where(take, size, 0)

    def fetch(i):
        each_part(i, lambda copy: copy.start())

    def scan(i, count):
        lidx[count] = i
        is_long = len_ref[base + i] > SHORT

        @pl.when(is_long & (count < SLOTS))
        def _():
            fetch(count)

        return count + jnp.where(is_long, 1, 0)

    n_long = lax.fori_loop(0, LOCAL, scan, jnp.int32(0))
    new_k.start()
    new_v.start()
    own = span(me, LOCAL)
    qf[...] = q_ref[...].astype(F32)
    knf[...] = kn_ref[own, :].astype(F32)
    vnf[...] = vn_ref[own, :].astype(F32)
    acc[...] = os_ref[...].astype(F32)

    def rows_of(ref, slot, rows):
        return jnp.concatenate([ref[slot, half, pl.ds(0, rows), :] for half in range(2)], axis=-1)

    def one_long(i, rows):
        seq = lidx[i]
        slot = i % SLOTS
        at = pl.ds(seq, 1)
        q8 = jnp.concatenate([qf[h, at, :] for h in range(HEADS)], axis=0)
        s = lax.dot_general(q8.astype(BF), rows_of(kl, slot, rows), DIMS_T, preferred_element_type=F32) * SCALE
        s = jnp.where(lax.broadcasted_iota(jnp.int32, s.shape, 1) < len_ref[base + seq], s, -jnp.inf)
        s_new = jnp.sum(q8 * knf[at, :], axis=-1, keepdims=True) * SCALE
        e, e_new, total = softmax_parts(s, s_new)
        num = jnp.dot(e, rows_of(vl, slot, rows), preferred_element_type=F32)
        return seq, (num + e_new * vnf[at, :]) / total

    def wait_and_clear(i, most):
        each_part(i, lambda copy: copy.wait())

        @pl.loop(chunks_of(i), most)
        def _(c):
            vl[i % SLOTS, :, span(c, CHUNK), :] = jnp.zeros((2, CHUNK, HALFW), BF)

    @pl.loop(0, (n_long + 1) // 2)
    def _(pair):
        a = pair * 2
        b = jnp.minimum(a + 1, n_long - 1)
        most = jnp.maximum(chunks_of(a), chunks_of(b))
        wait_and_clear(a, most)

        @pl.when(b > a)
        def _():
            wait_and_clear(b, most)

        for n in range(1, MAXLEN // CHUNK + 1):
            @pl.when(most == n)
            def _():
                results = [one_long(i, n * CHUNK) for i in (a, b)]
                for seq, out in results:
                    for h in range(HEADS):
                        acc[h, pl.ds(seq, 1), :] = out[h:h + 1, :]

        for i in (a, a + 1):
            @pl.when(i + SLOTS < n_long)
            def _():
                fetch(i + SLOTS)

    o_ref[...] = acc[...].astype(BF)
    new_k.wait()
    new_v.wait()


def attend(lengths, q, k_new, v_new, o_short, k_cache, v_cache):
    rows = k_new.shape[0]
    any_spec = pl.BlockSpec(memory_space=pl.ANY)
    vmem_spec = pl.BlockSpec(memory_space=pltpu.VMEM)
    return pl.pallas_call(
        attend_kernel,
        out_shape=(
            jax.ShapeDtypeStruct((HEADS, LOCAL, HD), BF),
            jax.ShapeDtypeStruct((rows, HD), BF),
            jax.ShapeDtypeStruct((rows, HD), BF),
        ),
        in_specs=[pl.BlockSpec(memory_space=pltpu.SMEM)] + [vmem_spec] * 4 + [any_spec] * 2,
        out_specs=(vmem_spec, any_spec, any_spec),
        scratch_shapes=[
            pltpu.VMEM((SLOTS, 2, MAXLEN, HALFW), BF),
            pltpu.VMEM((SLOTS, 2, MAXLEN, HALFW), BF),
            pltpu.VMEM((HEADS, LOCAL, HD), F32),
            pltpu.VMEM((LOCAL, HD), F32),
            pltpu.VMEM((LOCAL, HD), F32),
            pltpu.VMEM((HEADS, LOCAL, HD), F32),
            pltpu.SMEM((LOCAL + 8,), jnp.int32),
            pltpu.SemaphoreType.DMA((SLOTS,)),
            pltpu.SemaphoreType.DMA((SLOTS,)),
            pltpu.SemaphoreType.DMA((2,)),
        ],
        compiler_params=pltpu.CompilerParams(vmem_limit_bytes=40 * MIB),
        cost_estimate=pl.CostEstimate(flops=4 * 10 ** 9, bytes_accessed=10 ** 7, transcendentals=10 ** 6),
        name="attend",
    )(lengths, q, k_new, v_new, o_short, k_cache, v_cache)


HALF = HEADS // 2
X, Y, D, S = 2, 4, 6, 1


def output_kernel(o_ref, wc_ref, x_hbm, y_ref, og, xc, load_sem, os, orr, ys, yr):
    me, _, _, k = coords()
    cols = pl.ds(pl.multiple_of(me * HD, HD), HD)
    load_x = pltpu.make_async_copy(x_hbm.at[:, cols], xc, load_sem)
    load_x.start()
    entry_barrier((X, Y, S))
    started = []

    def o_copy(owner_rel, half, to, index):
        owner = peer(owner_rel)
        part = pl.ds(0, HEADS) if half is None else pl.ds(half * HALF, HALF)
        ref = og.at[owner, part]
        return remote(o_ref.at[part] if owner_rel == 0 else ref, ref, os.at[index], orr.at[index], to)

    def go(copy):
        copy.start()
        started.append(copy)

    def recv_o(owner_rel, half, to, index):
        o_copy(owner_rel, half, to, index).wait_recv()

    go(o_copy(0, 0, X, 0))
    go(o_copy(0, 1, Y, 1))
    go(o_copy(0, 1, X, 2))
    go(o_copy(0, 0, Y, 3))
    go(o_copy(0, None, S, 4))

    og[me] = o_ref[...]
    load_x.wait()

    def y_copy(col_rel, chip_rel, core, to, index):
        column = peer(col_rel)
        chip = peer(chip_rel) // 2
        first = chip * 2 + (0 if core is None else core)
        rows = pl.ds(pl.multiple_of(first * LOCAL, LOCAL), LOCAL if core is not None else 2 * LOCAL)
        ref = y_ref.at[rows, pl.ds(pl.multiple_of(column * HD, HD), HD)]
        return remote(ref, ref, ys.at[index], yr.at[index], to)

    def compute(step, chip_rel):
        chip = peer(chip_rel) // 2
        total = jnp.zeros((2 * LOCAL, HD), F32)
        for h in range(HEADS):
            lhs = og[pl.ds(chip * 2, 2), h].reshape(2 * LOCAL, HD)
            total = total + jnp.dot(lhs, wc_ref[pl.ds(h * HD, HD), :], preferred_element_type=F32)
        rows = pl.ds(pl.multiple_of(chip * 2 * LOCAL, 2 * LOCAL), 2 * LOCAL)
        y_ref[rows, cols] = (xc[rows, :].astype(F32) + total).astype(BF)
        b = step * 11
        go(y_copy(0, chip_rel, 0, X, b + 0))
        go(y_copy(0, chip_rel, 1, Y, b + 1))
        go(y_copy(0, chip_rel, 1, X, b + 2))
        go(y_copy(0, chip_rel, 0, Y, b + 3))
        go(y_copy(0, chip_rel, None, S, b + 4))

    recv_o(S, None, S, 4)
    compute(0, 0)
    recv_o(X, 0, X, 0)
    go(o_copy(X, 0, Y, 5))
    recv_o(Y, 1, Y, 1)
    go(o_copy(Y, 1, X, 6))
    recv_o(X, 1, X, 2)
    go(o_copy(X, None, S, 7))
    recv_o(Y, 0, Y, 3)
    go(o_copy(Y, None, S, 8))
    recv_o(X + S, None, S, 7)
    compute(1, X)
    recv_o(Y + S, None, S, 8)
    compute(2, Y)
    recv_o(D, 0, Y, 5)
    go(o_copy(D, 0, S, 9))
    recv_o(D, 1, X, 6)
    go(o_copy(D, 1, S, 10))
    recv_o(D + S, 0, S, 9)
    recv_o(D + S, 1, S, 10)
    compute(3, D)

    def xor(a, b):
        return ((a // 4 + b // 4) % 2) * 4 + ((a // 2 + b // 2) % 2) * 2 + (a + b) % 2

    order = (0, X, Y, D)
    for step, rel in enumerate(order):
        b = step * 11
        at_x, at_y, at_d = xor(rel, X), xor(rel, Y), xor(rel, D)
        y_copy(X, at_x, 0, X, b + 0).wait_recv()
        go(y_copy(X, at_x, 0, Y, b + 5))
        y_copy(Y, at_y, 1, Y, b + 1).wait_recv()
        go(y_copy(Y, at_y, 1, X, b + 6))
        y_copy(X, at_x, 1, X, b + 2).wait_recv()
        go(y_copy(X, at_x, None, S, b + 7))
        y_copy(Y, at_y, 0, Y, b + 3).wait_recv()
        go(y_copy(Y, at_y, None, S, b + 8))
    for step, rel in enumerate(order):
        b = step * 11
        at_d = xor(rel, D)
        y_copy(D, at_d, 0, Y, b + 5).wait_recv()
        go(y_copy(D, at_d, 0, S, b + 9))
        y_copy(D, at_d, 1, X, b + 6).wait_recv()
        go(y_copy(D, at_d, 1, S, b + 10))
    for step, rel in enumerate(order):
        b = step * 11
        at_x, at_y, at_d = xor(rel, X), xor(rel, Y), xor(rel, D)
        y_copy(S, rel, None, S, b + 4).wait_recv()
        y_copy(X + S, at_x, None, S, b + 7).wait_recv()
        y_copy(Y + S, at_y, None, S, b + 8).wait_recv()
        y_copy(D + S, at_d, 0, S, b + 9).wait_recv()
        y_copy(D + S, at_d, 1, S, b + 10).wait_recv()
    for copy in started:
        copy.wait_send()


def output(o, wc, x):
    rows, width = x.shape
    hbm_spec = pl.BlockSpec(memory_space=pltpu.HBM)
    vmem_spec = pl.BlockSpec(memory_space=pltpu.VMEM)
    return pl.pallas_call(
        output_kernel,
        out_shape=jax.ShapeDtypeStruct((rows, width), BF),
        in_specs=[vmem_spec, vmem_spec, hbm_spec],
        out_specs=vmem_spec,
        scratch_shapes=[
            pltpu.VMEM((8, HEADS, LOCAL, HD), BF),
            pltpu.VMEM((rows, HD), BF),
            pltpu.SemaphoreType.DMA,
            pltpu.SemaphoreType.DMA((11,)),
            pltpu.SemaphoreType.DMA((11,)),
            pltpu.SemaphoreType.DMA((44,)),
            pltpu.SemaphoreType.DMA((44,)),
        ],
        compiler_params=pltpu.CompilerParams(collective_id=1, has_side_effects=True, vmem_limit_bytes=40 * 2 ** 20),
        name="output",
    )(o, wc, x)


def solution(mesh):
    def local_step(x, w_query, w_key, w_value, w_out, k_cache, v_cache, lengths):
        x, w_query, w_key, w_value, w_out = (
            pltpu.with_memory_space_constraint(a, pltpu.HBM) for a in (x, w_query, w_key, w_value, w_out))
        q, k_new, v_new, w_cols, o_short = project(lengths, x, w_query, w_key, w_value, w_out, k_cache, v_cache)
        o, k_new, v_new = attend(lengths, q, k_new, v_new, o_short, k_cache, v_cache)
        y = output(o, w_cols, x)
        return y, k_new[:, None, :], v_new[:, None, :]

    rows_spec = P("replica")
    return jax.shard_map(
        local_step,
        mesh=mesh,
        in_specs=(P("replica", None), P(None, "model"), P(), P(), P("model", None), rows_spec, rows_spec, rows_spec),
        out_specs=(rows_spec, rows_spec, rows_spec),
        check_vma=False,
    )
```

time: 62.1 us -> 54.5 us (0.88); the launches traced: 62.2 us -> 55.6 us
  local copies, waits for them, and re-layouts: 7.81 us -> 2 us
  Pallas kernels: 53.7 us -> 52.9 us
    unnamed x15 -> x3, local copies, waits for them, and re-layouts: 7.81 us -> 2 us
    pallas_call x1, Pallas kernels: 24.9 us -> 23.4 us  [output(): pl.pallas_call(output_kernel, out_shape=jax.ShapeDtypeStruct((rows, width...]
    pallas_call x1, Pallas kernels: 20.8 us -> 22 us  [project(): pl.pallas_call(project_kernel, out_shape=(jax.ShapeDtypeStruct((HEADS, LO...]
where the time goes in v2:
time: 54.5 us; the launch traced here: 55.6 us
  Pallas kernels  52.9 us (97%)
  local copies, waits for them, and re-layouts  2 us (4%)
  between operations  0.66 us (1%)
    pallas_call x1, Pallas kernels, output(): pl.pallas_call(output_kernel, out_shape=jax.ShapeDtypeStruct((rows, width...  23.4 us
    pallas_call x1, Pallas kernels, project(): pl.pallas_call(project_kernel, out_shape=(jax.ShapeDtypeStruct((HEADS, LO...  22 us
    pallas_call x1, Pallas kernels, attend(): pl.pallas_call(attend_kernel, out_shape=(jax.ShapeDtypeStruct((HEADS, LOC...  7.45 us
    unnamed x3, local copies, waits for them, and re-layouts  2 us

profile of v2, /device:TPU:0, one launch (start us, length us, event | category | flops | bytes accessed | tf_op | source)
XLA Modules:
  0.0 55.6 jit_solution(11296378058264688783)
XLA Ops:
  0.6 0.0 copy-start
  0.6 0.7 %copy-done = s32[512]{0:T(512)S(1)} copy-done((s32[512]{0:T(512)S(1)}, s32[512]{0:T(512)}, u32[]{:S(2)}) %copy-start) | copy-done | bytes 2072
  1.3 22.0 %project.1 = (bf16[8,64,256]{2,1,0:T(8,128)(2,1)S(1)}, bf16[512,256]{1,0:T(8,128)(2,1)S(1)}, bf16[512,256]{1,0:T(8,128)(2,1)S(1)}, bf16[2048,256]{1,0:T(8,128)(2,1)S(1)}, bf16[8,64,256]{2,1,0:T(8,128)(2,1)S(1)}) custom-call(s32[512]{0:T(512)S(1)} %copy-done, bf16[512,2048]{1,0:T(8,128)(2,1)} %x_hbm.3, bf16[2048,256]{1,0:T(8,128)(2,1)} %wq_hbm.1, ...), custom_call_target="tpu_custom_call" | custom-call | tf_op jit(solution)/shard_map/project/pallas_call | solution.py:143
  23.4 7.5 %attend.1 = (bf16[8,64,256]{2,1,0:T(8,128)(2,1)S(1)}, bf16[512,256]{1,0:T(8,128)(2,1)}, bf16[512,256]{1,0:T(8,128)(2,1)}) custom-call(s32[512]{0:T(512)S(1)} %copy-done, bf16[8,64,256]{2,1,0:T(8,128)(2,1)S(1)} %get-tuple-element.11.q_ref, bf16[512,256]{1,0:T(8,128)(2,1)S(1)} %get-tuple-element.12.kn_ref, bf16[512,256]{1,0:T(8,128)(2,1)S(1)} %get-tuple-element.13.vn_ref, ...), custom_call_target="tpu_custom_call" | custom-call | flops 4000000000 | bytes 10000000 | tf_op jit(solution)/shard_map/attend/pallas_call | solution.py:280
  30.8 23.4 %output.1 = bf16[512,2048]{1,0:T(8,128)(2,1)S(1)} custom-call(bf16[8,64,256]{2,1,0:T(8,128)(2,1)S(1)} %get-tuple-element.15.o_ref, bf16[2048,256]{1,0:T(8,128)(2,1)S(1)} %get-tuple-element.16.wc_ref, bf16[512,2048]{1,0:T(8,128)(2,1)} %x_hbm.3), custom_call_target="tpu_custom_call" | custom-call | tf_op jit(solution)/shard_map/output/pallas_call | solution.py:424
  54.2 1.3 %copy.12 = bf16[512,2048]{1,0:T(8,128)(2,1)} copy(bf16[512,2048]{1,0:T(8,128)(2,1)S(1)} %output.1) | data formatting | bytes 4194304
Async XLA Ops:
  0.6 0.7 %copy-start = (s32[512]{0:T(512)S(1)}, s32[512]{0:T(512)}, u32[]{:S(2)}) copy-start(s32[512]{0:T(512)} %len_ref.3) | copy-start | bytes 6148

commit v3 on v2

--- a/solution.py
+++ b/solution.py
@@ -14,7 +14,8 @@
 GROUP = 16
 CHUNK = 256
 MAXLEN = 2048
-SLOTS = 14
+SLOTS = 6
+AHEAD = 4
 HALFW = 128
 MIB = 2 ** 20
 SCALE = HD ** -0.5
@@ -60,8 +61,8 @@
     return e.astype(BF), e_new.astype(BF).astype(F32), total
 
 
-def project_kernel(len_ref, x_hbm, wq_hbm, wk_hbm, wv_hbm, wo_hbm, k_hbm, v_hbm, q_out, kn_out, vn_out, wc_out, o_out,
-                   x_v, wq_v, wk_v, wv_v, q_v, ks, vs, lens_v, in_sem, own_sem, qs, qr, ws, wr):
+def project_kernel(len_hbm, x_hbm, wq_hbm, wk_hbm, wv_hbm, wo_hbm, k_hbm, v_hbm, q_out, kn_out, vn_out, wc_out, o_out, wx_out, wy_out,
+                   x_v, wq_v, wk_v, wv_v, wo_v, q_v, ks, vs, lens_v, len_ref, in_sem, own_sem, qs, qr, ws, wr):
     me, y, x, k = coords()
     mine = span(me, LOCAL)
     loads = [pltpu.make_async_copy(src, dst, in_sem.at[i]) for i, (src, dst) in enumerate((
@@ -71,9 +72,12 @@
         (wv_hbm, wv_v),
         (k_hbm.at[mine, 0, pl.ds(0, SHORT), :], ks),
         (v_hbm.at[mine, 0, pl.ds(0, SHORT), :], vs),
+        (len_hbm, len_ref),
+        (wo_hbm, wo_v),
     ))]
     loads[0].start()
     loads[1].start()
+    loads[7].start()
     entry_barrier(RELS)
     loads[0].wait()
     loads[1].wait()
@@ -87,13 +91,17 @@
             copy = remote(q_v.at[span(peer(rel), LOCAL), :], q_out.at[me], qs.at[rel], qr.at[rel], rel)
             copy.start()
             q_copies.append(copy)
-    for rel in RELS:
-        copy = remote(wo_hbm.at[:, span(peer(rel), HD)], wc_out.at[span(me, HD), :], ws.at[rel], wr.at[rel], rel)
+    loads[7].wait()
+    for rel in (6, 7, 1):
+        copy = remote(wo_v.at[:, span(peer(rel), HD)], wc_out.at[span(me, HD), :], ws.at[rel], wr.at[rel], rel)
         copy.start()
         w_copies.append(copy)
-    own_w = pltpu.make_async_copy(wo_hbm.at[:, span(me, HD)], wc_out.at[span(me, HD), :], own_sem)
-    own_w.start()
-    for load in loads[2:]:
+    stores = [pltpu.make_async_copy(wo_v.at[:, span(peer(rel) // 2, 2 * HD)], out, own_sem.at[i])
+              for i, (rel, out) in enumerate(((X, wx_out), (Y, wy_out)))]
+    for store in stores:
+        store.start()
+    wc_out[span(me, HD), :] = wo_v[:, span(me, HD)]
+    for load in loads[2:7]:
         load.start()
     q_out[me] = q_v[mine, :]
 
@@ -101,8 +109,9 @@
         lens_v[pl.ds(i, 1), :] = jnp.full((1, 128), len_ref[me * LOCAL + i], jnp.int32)
         return carry
 
+    loads[6].wait()
     lax.fori_loop(0, LOCAL, spread, 0)
-    for load in loads[2:]:
+    for load in loads[2:6]:
         load.wait()
     for part in range(2):
         rows = pl.ds(part * 256, 256)
@@ -131,8 +140,7 @@
         return carry
 
     lax.fori_loop(0, LOCAL // GROUP, group, 0)
-    own_w.wait()
-    for copy in w_copies:
+    for copy in w_copies + stores:
         copy.wait()
 
 
@@ -148,20 +156,24 @@
             jax.ShapeDtypeStruct((rows, HD), BF),
             jax.ShapeDtypeStruct((HEADS * HD, HD), BF),
             jax.ShapeDtypeStruct((HEADS, LOCAL, HD), BF),
+            jax.ShapeDtypeStruct((HD, 2 * HD), BF),
+            jax.ShapeDtypeStruct((HD, 2 * HD), BF),
         ),
-        in_specs=[pl.BlockSpec(memory_space=pltpu.SMEM)] + [hbm_spec] * 7,
-        out_specs=(vmem_spec,) * 5,
+        in_specs=[hbm_spec] * 8,
+        out_specs=(vmem_spec,) * 5 + (hbm_spec,) * 2,
         scratch_shapes=[
             pltpu.VMEM((rows, depth), BF),
             pltpu.VMEM((depth, HD), BF),
             pltpu.VMEM((depth, HD), BF),
             pltpu.VMEM((depth, HD), BF),
+            pltpu.VMEM(wo.shape, BF),
             pltpu.VMEM((rows, HD), BF),
             pltpu.VMEM((LOCAL, SHORT, HD), BF),
             pltpu.VMEM((LOCAL, SHORT, HD), BF),
             pltpu.VMEM((LOCAL, 128), jnp.int32),
-            pltpu.SemaphoreType.DMA((6,)),
-            pltpu.SemaphoreType.DMA,
+            pltpu.SMEM(lengths.shape, jnp.int32),
+            pltpu.SemaphoreType.DMA((8,)),
+            pltpu.SemaphoreType.DMA((2,)),
             pltpu.SemaphoreType.DMA((8,)),
             pltpu.SemaphoreType.DMA((8,)),
             pltpu.SemaphoreType.DMA((8,)),
@@ -173,43 +185,41 @@
 
 
 def attend_kernel(len_ref, q_ref, kn_ref, vn_ref, os_ref, k_hbm, v_hbm, o_ref, kn_out, vn_out,
-                  kl, vl, qf, knf, vnf, acc, lidx, k_sem, v_sem, new_sem):
+                  kl, vl, qf, knf, vnf, acc, lidx, lchunks, k_sem, v_sem, new_sem):
     me = lax.axis_index("model")
     base = me * LOCAL
     new_k = pltpu.make_async_copy(kn_ref, kn_out, new_sem.at[0])
     new_v = pltpu.make_async_copy(vn_ref, vn_out, new_sem.at[1])
 
-    def chunks_of(i):
-        return (len_ref[base + lidx[i]] + CHUNK - 1) // CHUNK
-
-    def each_part(i, action):
-        slot = i % SLOTS
-        chunks = chunks_of(i)
-        first = jnp.int32(0)
+    def each_part(i, slot, action):
+        seq = base + lidx[i]
+        chunks = lchunks[i]
+        first = 0
         for size in (8, 4, 2, 1):
-            take = chunks - first >= size
             rows = pl.ds(pl.multiple_of(first * CHUNK, CHUNK), size * CHUNK)
 
-            @pl.when(take)
+            @pl.when(chunks & size != 0)
             def _():
                 for cache, dst, sem in ((k_hbm, kl, k_sem), (v_hbm, vl, v_sem)):
                     for half in range(2):
                         action(pltpu.make_async_copy(
-                            cache.at[base + lidx[i], 0, rows, pl.ds(half * HALFW, HALFW)],
+                            cache.at[seq, 0, rows, pl.ds(half * HALFW, HALFW)],
                             dst.at[slot, half, rows, :], sem.at[slot]))
 
-            first = first + jnp.where(take, size, 0)
-
-    def fetch(i):
-        each_part(i, lambda copy: copy.start())
+            first = first + (chunks & size)
+
+    def fetch(i, slot):
+        each_part(i, slot, lambda copy: copy.start())
 
     def scan(i, count):
+        length = len_ref[base + i]
         lidx[count] = i
-        is_long = len_ref[base + i] > SHORT
-
-        @pl.when(is_long & (count < SLOTS))
+        lchunks[count] = jnp.right_shift(length + (CHUNK - 1), CHUNK.bit_length() - 1)
+        is_long = length > SHORT
+
+        @pl.when(is_long & (count < AHEAD))
         def _():
-            fetch(count)
+            fetch(count, count)
 
         return count + jnp.where(is_long, 1, 0)
 
@@ -225,9 +235,8 @@
     def rows_of(ref, slot, rows):
         return jnp.concatenate([ref[slot, half, pl.ds(0, rows), :] for half in range(2)], axis=-1)
 
-    def one_long(i, rows):
+    def one_long(i, slot, rows):
         seq = lidx[i]
-        slot = i % SLOTS
         at = pl.ds(seq, 1)
         q8 = jnp.concatenate([qf[h, at, :] for h in range(HEADS)], axis=0)
         s = lax.dot_general(q8.astype(BF), rows_of(kl, slot, rows), DIMS_T, preferred_element_type=F32) * SCALE
@@ -237,37 +246,42 @@
         num = jnp.dot(e, rows_of(vl, slot, rows), preferred_element_type=F32)
         return seq, (num + e_new * vnf[at, :]) / total
 
-    def wait_and_clear(i, most):
-        each_part(i, lambda copy: copy.wait())
-
-        @pl.loop(chunks_of(i), most)
+    def wait_and_clear(i, slot, most):
+        each_part(i, slot, lambda copy: copy.wait())
+
+        @pl.loop(lchunks[i], most)
         def _(c):
-            vl[i % SLOTS, :, span(c, CHUNK), :] = jnp.zeros((2, CHUNK, HALFW), BF)
-
-    @pl.loop(0, (n_long + 1) // 2)
-    def _(pair):
+            vl[slot, :, span(c, CHUNK), :] = jnp.zeros((2, CHUNK, HALFW), BF)
+
+    def step(pair, slot):
         a = pair * 2
-        b = jnp.minimum(a + 1, n_long - 1)
-        most = jnp.maximum(chunks_of(a), chunks_of(b))
-        wait_and_clear(a, most)
-
-        @pl.when(b > a)
+        alone = a + 1 >= n_long
+        b = jnp.where(alone, a, a + 1)
+        slot_b = jnp.where(alone, slot, slot + 1)
+        most = jnp.maximum(lchunks[a], lchunks[b])
+        wait_and_clear(a, slot, most)
+
+        @pl.when(jnp.logical_not(alone))
         def _():
-            wait_and_clear(b, most)
+            wait_and_clear(b, slot + 1, most)
+
+        later = jnp.where(slot >= SLOTS - AHEAD, slot + AHEAD - SLOTS, slot + AHEAD)
+        for j in range(2):
+            @pl.when(a + AHEAD + j < n_long)
+            def _():
+                fetch(a + AHEAD + j, later + j)
 
         for n in range(1, MAXLEN // CHUNK + 1):
             @pl.when(most == n)
             def _():
-                results = [one_long(i, n * CHUNK) for i in (a, b)]
+                results = [one_long(i, at, n * CHUNK) for i, at in ((a, slot), (b, slot_b))]
                 for seq, out in results:
                     for h in range(HEADS):
                         acc[h, pl.ds(seq, 1), :] = out[h:h + 1, :]
 
-        for i in (a, a + 1):
-            @pl.when(i + SLOTS < n_long)
-            def _():
-                fetch(i + SLOTS)
-
+        return jnp.where(slot + 2 >= SLOTS, 0, slot + 2)
+
+    lax.fori_loop(0, jnp.right_shift(n_long + 1, 1), step, jnp.int32(0))
     o_ref[...] = acc[...].astype(BF)
     new_k.wait()
     new_v.wait()
@@ -294,11 +308,12 @@
             pltpu.VMEM((LOCAL, HD), F32),
             pltpu.VMEM((HEADS, LOCAL, HD), F32),
             pltpu.SMEM((LOCAL + 8,), jnp.int32),
+            pltpu.SMEM((LOCAL + 8,), jnp.int32),
             pltpu.SemaphoreType.DMA((SLOTS,)),
             pltpu.SemaphoreType.DMA((SLOTS,)),
             pltpu.SemaphoreType.DMA((2,)),
         ],
-        compiler_params=pltpu.CompilerParams(vmem_limit_bytes=40 * MIB),
+        compiler_params=pltpu.CompilerParams(vmem_limit_bytes=24 * MIB),
         cost_estimate=pl.CostEstimate(flops=4 * 10 ** 9, bytes_accessed=10 ** 7, transcendentals=10 ** 6),
         name="attend",
     )(lengths, q, k_new, v_new, o_short, k_cache, v_cache)
@@ -308,11 +323,19 @@
 X, Y, D, S = 2, 4, 6, 1
 
 
-def output_kernel(o_ref, wc_ref, x_hbm, y_ref, og, xc, load_sem, os, orr, ys, yr):
+def output_kernel(o_ref, wc_ref, wx_hbm, wy_hbm, x_hbm, y_ref, og, xc, wp, load_sem, wss, wrs, os, orr, ys, yr):
     me, _, _, k = coords()
+    other = peer(S) % 2
+    w_loads, w_copies, w_recvs = [], [], []
+    for i, (rel, ref) in enumerate(((X, wx_hbm), (Y, wy_hbm))):
+        w_loads.append(pltpu.make_async_copy(ref.at[:, span(k, HD)], wp.at[2 * i + k], load_sem.at[1 + i]))
+        w_copies.append(remote(ref.at[:, span(other, HD)], wp.at[2 * i + k], wss.at[i], wrs.at[i], S))
+        w_recvs.append(remote(ref.at[:, span(other, HD)], wp.at[2 * i + other], wss.at[i], wrs.at[i], S))
     cols = pl.ds(pl.multiple_of(me * HD, HD), HD)
-    load_x = pltpu.make_async_copy(x_hbm.at[:, cols], xc, load_sem)
+    load_x = pltpu.make_async_copy(x_hbm.at[:, cols], xc, load_sem.at[0])
     load_x.start()
+    for load in w_loads:
+        load.start()
     entry_barrier((X, Y, S))
     started = []
 
@@ -334,9 +357,15 @@
     go(o_copy(0, 1, X, 2))
     go(o_copy(0, 0, Y, 3))
     go(o_copy(0, None, S, 4))
+    for c in w_copies:
+        go(c)
 
     og[me] = o_ref[...]
     load_x.wait()
+    for load in w_loads:
+        load.wait()
+    for c in w_recvs:
+        c.wait_recv()
 
     def y_copy(col_rel, chip_rel, core, to, index):
         column = peer(col_rel)
@@ -349,9 +378,12 @@
     def compute(step, chip_rel):
         chip = peer(chip_rel) // 2
         total = jnp.zeros((2 * LOCAL, HD), F32)
-        for h in range(HEADS):
-            lhs = og[pl.ds(chip * 2, 2), h].reshape(2 * LOCAL, HD)
-            total = total + jnp.dot(lhs, wc_ref[pl.ds(h * HD, HD), :], preferred_element_type=F32)
+        for i, head_rel in enumerate((0, D, X, Y)):
+            for j in range(2):
+                head = peer(head_rel) // 2 * 2 + j
+                lhs = og[pl.ds(chip * 2, 2), head].reshape(2 * LOCAL, HD)
+                rhs = wc_ref[span(head, HD), :] if i < 2 else wp[2 * (i - 2) + j]
+                total = total + jnp.dot(lhs, rhs, preferred_element_type=F32)
         rows = pl.ds(pl.multiple_of(chip * 2 * LOCAL, 2 * LOCAL), 2 * LOCAL)
         y_ref[rows, cols] = (xc[rows, :].astype(F32) + total).astype(BF)
         b = step * 11
@@ -417,36 +449,41 @@
         copy.wait_send()
 
 
-def output(o, wc, x):
+def output(o, wc, wx, wy, x):
     rows, width = x.shape
     hbm_spec = pl.BlockSpec(memory_space=pltpu.HBM)
     vmem_spec = pl.BlockSpec(memory_space=pltpu.VMEM)
     return pl.pallas_call(
         output_kernel,
         out_shape=jax.ShapeDtypeStruct((rows, width), BF),
-        in_specs=[vmem_spec, vmem_spec, hbm_spec],
+        in_specs=[vmem_spec, vmem_spec, hbm_spec, hbm_spec, hbm_spec],
         out_specs=vmem_spec,
         scratch_shapes=[
             pltpu.VMEM((8, HEADS, LOCAL, HD), BF),
             pltpu.VMEM((rows, HD), BF),
-            pltpu.SemaphoreType.DMA,
+            pltpu.VMEM((4, HD, HD), BF),
+            pltpu.SemaphoreType.DMA((3,)),
+            pltpu.SemaphoreType.DMA((2,)),
+            pltpu.SemaphoreType.DMA((2,)),
             pltpu.SemaphoreType.DMA((11,)),
             pltpu.SemaphoreType.DMA((11,)),
             pltpu.SemaphoreType.DMA((44,)),
             pltpu.SemaphoreType.DMA((44,)),
         ],
-        compiler_params=pltpu.CompilerParams(collective_id=1, has_side_effects=True, vmem_limit_bytes=40 * 2 ** 20),
+        compiler_params=pltpu.CompilerParams(collective_id=1, has_side_effects=True, vmem_limit_bytes=24 * MIB),
         name="output",
-    )(o, wc, x)
+    )(o, wc, wx, wy, x)
 
 
 def solution(mesh):
     def local_step(x, w_query, w_key, w_value, w_out, k_cache, v_cache, lengths):
         x, w_query, w_key, w_value, w_out = (
             pltpu.with_memory_space_constraint(a, pltpu.HBM) for a in (x, w_query, w_key, w_value, w_out))
-        q, k_new, v_new, w_cols, o_short = project(lengths, x, w_query, w_key, w_value, w_out, k_cache, v_cache)
+        pinned = pltpu.with_memory_space_constraint(lengths, pltpu.HBM)
+        q, k_new, v_new, w_cols, o_short, wx, wy = project(pinned, x, w_query, w_key, w_value, w_out, k_cache, v_cache)
+        wx, wy = (lax.ppermute(w, "model", [(d, d ^ rel) for d in range(8)]) for w, rel in ((wx, X), (wy, Y)))
         o, k_new, v_new = attend(lengths, q, k_new, v_new, o_short, k_cache, v_cache)
-        y = output(o, w_cols, x)
+        y = output(o, w_cols, wx, wy, x)
         return y, k_new[:, None, :], v_new[:, None, :]
 
     rows_spec = P("replica")

time: 54.5 us -> 51.2 us (0.939); the launches traced: 55.6 us -> 51.3 us
  Pallas kernels: 52.9 us -> 47 us
  starting transfers between devices: 0 us -> 2.35 us
  local copies, waits for them, and re-layouts: 2 us -> 1.33 us
    pallas_call x1, Pallas kernels: 22 us -> 15.9 us  [project(): pl.pallas_call(project_kernel, out_shape=(jax.ShapeDtypeStruct((HEADS, LO...]
    ppermute x0 -> x2, starting transfers between devices: none -> 2.35 us  [local_step(): lax.ppermute(w, 'model', [(d, d ^ rel) for d in range(8)])]
    pallas_call x1, Pallas kernels: 7.45 us -> 8.76 us  [attend(): pl.pallas_call(attend_kernel, out_shape=(jax.ShapeDtypeStruct((HEADS, LOC...]
    pallas_call x1, Pallas kernels: 23.4 us -> 22.3 us  [output(): pl.pallas_call(output_kernel, out_shape=jax.ShapeDtypeStruct((rows, width...]
    unnamed x3, local copies, waits for them, and re-layouts: 2 us -> 1.33 us
  transfers between devices with their start and end apart: 0 -> 2, of which waited for: 0 -> 0; matrix products, arithmetic and copies ran while one was open for 0% -> 0% of each run, Pallas kernels for 0% -> 17%
where the time goes in v3:
time: 51.2 us; the launch traced here: 51.3 us
  Pallas kernels  47 us (92%)
  starting transfers between devices  2.35 us (5%)
  local copies, waits for them, and re-layouts  1.33 us (3%)
  between operations  0.69 us (1%)
    pallas_call x1, Pallas kernels, output(): pl.pallas_call(output_kernel, out_shape=jax.ShapeDtypeStruct((rows, width...  22.3 us
    pallas_call x1, Pallas kernels, project(): pl.pallas_call(project_kernel, out_shape=(jax.ShapeDtypeStruct((HEADS, LO...  15.9 us
    pallas_call x1, Pallas kernels, attend(): pl.pallas_call(attend_kernel, out_shape=(jax.ShapeDtypeStruct((HEADS, LOC...  8.76 us
    ppermute x2, starting transfers between devices, local_step(): lax.ppermute(w, 'model', [(d, d ^ rel) for d in range(8)])  2.35 us
    unnamed x3, local copies, waits for them, and re-layouts  1.33 us
  transfers between devices with their start and end apart: 2, of which 0 were waited for; matrix products, arithmetic and copies ran while one was open for 0% of the time, Pallas kernels for 17%

profile of v3, /device:TPU:0, one launch (start us, length us, event | category | flops | bytes accessed | tf_op | source)
XLA Modules:
  0.0 51.3 jit_solution(3021741702044943826)
XLA Ops:
  0.6 0.0 copy-start
  0.6 15.9 %project.1 = (bf16[8,64,256]{2,1,0:T(8,128)(2,1)S(1)}, bf16[512,256]{1,0:T(8,128)(2,1)S(1)}, bf16[512,256]{1,0:T(8,128)(2,1)S(1)}, bf16[2048,256]{1,0:T(8,128)(2...) custom-call(s32[512]{0:T(512)} %len_ref.1, bf16[512,2048]{1,0:T(8,128)(2,1)} %x_hbm.3, ...), custom_call_target="tpu_custom_call" | custom-call | tf_op jit(solution)/shard_map/project/pallas_call | solution.py:151
  16.5 0.0 collective-permute-start
  16.6 2.3 %collective-permute-start.1 = (bf16[256,512]{1,0:T(8,128)(2,1)}, bf16[256,512]{1,0:T(8,128)(2,1)}, u32[]{:S(2)}, u32[]{:S(2)}) collective-permute-start(bf16[256,512]{1,0:T(8,128)(2,1)} %get-tuple-element.20), channel_id=1, source_target_pairs={{0,4},{1,5},{2,6},{3,7},{4,0},{5,1},{6,2},{7,3}} | collective-permute-start | bytes 786440 | tf_op jit(solution)/shard_map/ppermute | solution.py:484
  18.9 0.0 copy-done
  18.9 8.8 %attend.1 = (bf16[8,64,256]{2,1,0:T(8,128)(2,1)S(1)}, bf16[512,256]{1,0:T(8,128)(2,1)}, bf16[512,256]{1,0:T(8,128)(2,1)}) custom-call(s32[512]{0:T(512)S(1)} %copy-done, bf16[8,64,256]{2,1,0:T(8,128)(2,1)S(1)} %get-tuple-element.13.q_ref, bf16[512,256]{1,0:T(8,128)(2,1)S(1)} %get-tuple-element.14.kn_ref, bf16[512,256]{1,0:T(8,128)(2,1)S(1)} %get-tuple-element.15.vn_ref, ...), custom_call_target="tpu_custom_call" | custom-call | flops 4000000000 | bytes 10000000 | tf_op jit(solution)/shard_map/attend/pallas_call | solution.py:294
  27.7 0.0 collective-permute-done.wx_hbm
  27.7 0.0 collective-permute-done.1.wy_hbm
  27.7 22.3 %output.1 = bf16[512,2048]{1,0:T(8,128)(2,1)S(1)} custom-call(bf16[8,64,256]{2,1,0:T(8,128)(2,1)S(1)} %get-tuple-element.17.o_ref, bf16[2048,256]{1,0:T(8,128)(2,1)S(1)} %get-tuple-element.18.wc_ref, bf16[256,512]{1,0:T(8,128)(2,1)} %collective-permute-done.wx_hbm, bf16[256,512]{1,0:T(8,128)(2,1)} %collective-permute-done.1.wy_hbm, bf16[512,2048]{1,0:T(8,128)(2,1)} %x_hbm.3), custom_call_target="tpu_custom_call" | custom-call | tf_op jit(solution)/shard_map/output/pallas_call | solution.py:456
  50.0 1.3 %copy.12 = bf16[512,2048]{1,0:T(8,128)(2,1)} copy(bf16[512,2048]{1,0:T(8,128)(2,1)S(1)} %output.1) | data formatting | bytes 4194304
Async XLA Ops:
  0.6 18.3 %copy-start = (s32[512]{0:T(512)S(1)}, s32[512]{0:T(512)}, u32[]{:S(2)}) copy-start(s32[512]{0:T(512)} %len_ref.1) | copy-start | bytes 6148
  16.5 11.1 %collective-permute-start = (bf16[256,512]{1,0:T(8,128)(2,1)}, bf16[256,512]{1,0:T(8,128)(2,1)}, u32[]{:S(2)}, u32[]{:S(2)}) collective-permute-start(bf16[256,512]{1,0:T(8,128)(2,1)} %get-tuple-element.19), channel_id=1, source_target_pairs={{0,2},{1,3},{2,0},{3,1},{4,6},{5,7},{6,4},{7,5}} | collective-permute-start | bytes 786440 | tf_op jit(solution)/shard_map/ppermute | solution.py:484
  16.6 11.1 %collective-permute-start.1 = (bf16[256,512]{1,0:T(8,128)(2,1)}, bf16[256,512]{1,0:T(8,128)(2,1)}, u32[]{:S(2)}, u32[]{:S(2)}) collective-permute-start(bf16[256,512]{1,0:T(8,128)(2,1)} %get-tuple-element.20), channel_id=1, source_target_pairs={{0,4},{1,5},{2,6},{3,7},{4,0},{5,1},{6,2},{7,3}} | collective-permute-start | bytes 786440 | tf_op jit(solution)/shard_map/ppermute | solution.py:484
